TPU v7x, 32 devices: a whole 2x2x4 slice. The times are simulated.
32 devices in a mesh: dp: 8 (over z, x), mp: 4 (over y, core).
Axes of the slice: x: 2, y: 2, z: 4, core: 2. Of those that a mesh axis runs over, the one named last changes fastest.
Arguments:
- tokens: bfloat16 [16384, 1024], P('dp'), may hold values from -6 to 6
- cotangent: bfloat16 [16384, 1024], P('dp'), may hold values from -15 to 15
- item_lengths: int32 [8, 8], P('dp'), may hold values from 1 to 1024, 2048 in all within a row
- w_qkv: bfloat16 [3, 1024, 1024], P(None, None, 'mp'), may hold values from -0.1875 to 0.1875
- b_qv: float32 [2, 1024], P(None, 'mp'), may hold values from -3 to 3
- w_out: bfloat16 [1024, 1024], P('mp'), may hold values from -0.75 to 0.75
- b_out: float32 [1024], replicated, may hold values from -1.75 to 1.75
- w_fc1: bfloat16 [1024, 4096], P(None, 'mp'), may hold values from -0.1875 to 0.1875
- b_fc1: float32 [4096], P('mp'), may hold values from -3 to 3
- w_fc2: bfloat16 [4096, 1024], P('mp'), may hold values from -0.09375 to 0.09375
- b_fc2: float32 [1024], replicated, may hold values from -1.75 to 1.75
- ln1_gain: float32 [1024], replicated, may hold values from 0.5 to 1.5
- ln1_bias: float32 [1024], replicated, may hold values from -1.75 to 1.75
- ln2_gain: float32 [1024], replicated, may hold values from 0.5 to 1.5
- ln2_bias: float32 [1024], replicated, may hold values from -1.75 to 1.75
Outputs:
- output: bfloat16 [16384, 1024], P('dp')
- grad_tokens: float32 [16384, 1024], P('dp')
- grad_w_qkv: float32 [3, 1024, 1024], P(None, 'dp', 'mp')
- grad_b_qv: float32 [2, 1024], P(None, 'mp')
- grad_w_out: float32 [1024, 1024], P('mp', 'dp')
- grad_b_out: float32 [1024], replicated
- grad_w_fc1: float32 [1024, 4096], P('dp', 'mp')
- grad_b_fc1: float32 [4096], P('mp')
- grad_w_fc2: float32 [4096, 1024], P('mp', 'dp')
- grad_b_fc2: float32 [1024], replicated
- grad_ln1_gain: float32 [1024], replicated
- grad_ln1_bias: float32 [1024], replicated
- grad_ln2_gain: float32 [1024], replicated
- grad_ln2_bias: float32 [1024], replicated
Inputs may be any that keep to these rules, and one draw needn't show every extreme that they name: `item_lengths`: each row sums to 2048, and each row's longest item has exactly 1024 patches.
All inputs are finite; a program needn't handle non-finite values.
Results may differ from a plain program's by a relative error of at most 0.019.
Values may be sent and summed in bfloat16 or wider, within the bound.
A program may use at most 192 MiB of HBM per device.

v0:
```python
from functools import partial
import jax
import jax.numpy as jnp
from jax import lax
from jax.sharding import PartitionSpec as P

HEAD = 64
QBLOCK = 512


def normalize(values, gain, shift):
    center = jnp.mean(values, axis=-1, keepdims=True)
    centered = values - center
    spread = jnp.mean(centered * centered, axis=-1, keepdims=True)
    return centered * lax.rsqrt(spread + 1e-06) * gain + shift


def exact_gelu(values):
    return jax.nn.gelu(values, approximate=False)


def segment_ids(lengths_row, row_count):
    ends = jnp.cumsum(lengths_row)
    positions = jnp.arange(row_count, dtype=jnp.int32)
    return jnp.sum((positions[:, None] >= ends[None, :]).astype(jnp.int32), axis=1)


def mp_allreduce(partial, n_mp):
    if n_mp != 4:
        return lax.psum(partial, "mp").astype(jnp.float32)
    idx = lax.axis_index("mp")
    low_bit = idx % 2
    half = partial.shape[0] // 2
    mine = lax.dynamic_slice_in_dim(partial, low_bit * half, half, 0)
    other = lax.dynamic_slice_in_dim(partial, (1 - low_bit) * half, half, 0)
    got = lax.ppermute(other, "mp", [(k, k ^ 1) for k in range(4)])
    first = (mine.astype(jnp.float32) + got.astype(jnp.float32)).astype(jnp.bfloat16)
    got_far = lax.ppermute(first, "mp", [(k, k ^ 2) for k in range(4)])
    second = (first.astype(jnp.float32) + got_far.astype(jnp.float32)).astype(jnp.bfloat16)
    got_back = lax.ppermute(second, "mp", [(k, k ^ 1) for k in range(4)])
    top = jnp.where(low_bit == 0, second, got_back)
    bottom = jnp.where(low_bit == 0, got_back, second)
    return jnp.concatenate([top, bottom], axis=0).astype(jnp.float32)


def per_device(
    n_mp,
    tokens,
    cotangent,
    item_lengths,
    w_qkv,
    b_qv,
    w_out,
    b_out,
    w_fc1,
    b_fc1,
    w_fc2,
    b_fc2,
    ln1_gain,
    ln1_bias,
    ln2_gain,
    ln2_bias,
):
    row_count = tokens.shape[0]
    local_cols = w_qkv.shape[2]
    heads_here = local_cols // HEAD
    blocks = row_count // QBLOCK
    score_scale = HEAD ** (-0.5)
    segments = segment_ids(item_lengths[0], row_count)
    seg_blocks = segments.reshape(blocks, QBLOCK)
    inputs = tokens.astype(jnp.float32)
    norm_one, norm_one_back = jax.vjp(normalize, inputs, ln1_gain, ln1_bias)
    normed_one = norm_one.astype(jnp.bfloat16)
    queries = (jnp.dot(normed_one, w_qkv[0], preferred_element_type=jnp.float32) + b_qv[0]).astype(
        jnp.bfloat16
    )
    key_rows = jnp.dot(normed_one, w_qkv[1], preferred_element_type=jnp.float32).astype(
        jnp.bfloat16
    )
    value_rows = (
        jnp.dot(normed_one, w_qkv[2], preferred_element_type=jnp.float32) + b_qv[1]
    ).astype(jnp.bfloat16)
    key_heads = key_rows.reshape(row_count, heads_here, HEAD)
    value_heads = value_rows.reshape(row_count, heads_here, HEAD)
    query_blocks = queries.reshape(blocks, QBLOCK, heads_here, HEAD)

    def block_scores(query_block, seg_block):
        scores = (
            jnp.einsum("qhd,khd->hqk", query_block, key_heads, preferred_element_type=jnp.float32)
            * score_scale
        )
        same = seg_block[:, None] == segments[None, :]
        return jnp.where(same[None], scores, -1e30)

    def forward_block(pieces):
        query_block, seg_block = pieces
        scores = block_scores(query_block, seg_block)
        row_max = jnp.max(scores, axis=-1, keepdims=True)
        raised = jnp.exp(scores - row_max)
        row_sum = jnp.sum(raised, axis=-1, keepdims=True)
        probs = raised / row_sum
        block_out = jnp.einsum(
            "hqk,khd->qhd",
            probs.astype(jnp.bfloat16),
            value_heads,
            preferred_element_type=jnp.float32,
        )
        return (block_out.astype(jnp.bfloat16), (row_max + jnp.log(row_sum))[..., 0])

    out_blocks, log_norms = lax.map(forward_block, (query_blocks, seg_blocks))
    attended = out_blocks.reshape(row_count, local_cols)
    attention_sum = mp_allreduce(
        jnp.dot(attended, w_out, preferred_element_type=jnp.float32).astype(jnp.bfloat16), n_mp
    )
    middle = inputs + attention_sum + b_out
    norm_two, norm_two_back = jax.vjp(normalize, middle, ln2_gain, ln2_bias)
    normed_two = norm_two.astype(jnp.bfloat16)
    hidden_pre = jnp.dot(normed_two, w_fc1, preferred_element_type=jnp.float32) + b_fc1
    activated_full, gelu_back = jax.vjp(exact_gelu, hidden_pre)
    activated = activated_full.astype(jnp.bfloat16)
    mlp_sum = mp_allreduce(
        jnp.dot(activated, w_fc2, preferred_element_type=jnp.float32).astype(jnp.bfloat16), n_mp
    )
    output = (middle + mlp_sum + b_fc2).astype(jnp.bfloat16)
    upstream = cotangent.astype(jnp.float32)
    grad_b_fc2 = jnp.sum(upstream, axis=0)
    grad_w_fc2 = jnp.einsum("tf,td->fd", activated, cotangent, preferred_element_type=jnp.float32)
    d_act = jnp.einsum("td,fd->tf", cotangent, w_fc2, preferred_element_type=jnp.float32)
    d_pre = gelu_back(d_act)[0]
    grad_b_fc1 = jnp.sum(d_pre, axis=0)
    d_pre_low = d_pre.astype(jnp.bfloat16)
    grad_w_fc1 = jnp.einsum("td,tf->df", normed_two, d_pre_low, preferred_element_type=jnp.float32)
    d_normed_two = mp_allreduce(
        jnp.einsum("tf,df->td", d_pre_low, w_fc1, preferred_element_type=jnp.float32).astype(
            jnp.bfloat16
        ),
        n_mp,
    )
    d_middle_norm, grad_ln2_gain, grad_ln2_bias = norm_two_back(d_normed_two)
    d_middle = upstream + d_middle_norm
    grad_b_out = jnp.sum(d_middle, axis=0)
    d_middle_low = d_middle.astype(jnp.bfloat16)
    grad_w_out = jnp.einsum("tc,td->cd", attended, d_middle_low, preferred_element_type=jnp.float32)
    d_attended = jnp.einsum(
        "td,cd->tc", d_middle_low, w_out, preferred_element_type=jnp.float32
    ).astype(jnp.bfloat16)
    d_att_blocks = d_attended.reshape(blocks, QBLOCK, heads_here, HEAD)

    def backward_block(running, pieces):
        d_keys_acc, d_values_acc = running
        query_block, seg_block, d_out_block, log_norm = pieces
        scores = block_scores(query_block, seg_block)
        probs = jnp.exp(scores - log_norm[..., None])
        d_probs = jnp.einsum(
            "qhd,khd->hqk", d_out_block, value_heads, preferred_element_type=jnp.float32
        )
        d_scores = probs * (d_probs - jnp.sum(probs * d_probs, axis=-1, keepdims=True))
        d_scores_low = d_scores.astype(jnp.bfloat16)
        d_query_block = (
            jnp.einsum("hqk,khd->qhd", d_scores_low, key_heads, preferred_element_type=jnp.float32)
            * score_scale
        )
        d_keys_acc = (
            d_keys_acc
            + jnp.einsum(
                "hqk,qhd->khd", d_scores_low, query_block, preferred_element_type=jnp.float32
            )
            * score_scale
        )
        d_values_acc = d_values_acc + jnp.einsum(
            "hqk,qhd->khd",
            probs.astype(jnp.bfloat16),
            d_out_block,
            preferred_element_type=jnp.float32,
        )
        return ((d_keys_acc, d_values_acc), d_query_block)

    zeros_acc = jnp.zeros((row_count, heads_here, HEAD), jnp.float32)
    (d_keys, d_values), d_query_blocks = lax.scan(
        backward_block, (zeros_acc, zeros_acc), (query_blocks, seg_blocks, d_att_blocks, log_norms)
    )
    d_queries = d_query_blocks.reshape(row_count, local_cols)
    d_keys = d_keys.reshape(row_count, local_cols)
    d_values = d_values.reshape(row_count, local_cols)
    grad_b_qv = jnp.stack([jnp.sum(d_queries, axis=0), jnp.sum(d_values, axis=0)])
    stacked = jnp.stack([d_queries, d_keys, d_values]).astype(jnp.bfloat16)
    grad_w_qkv = jnp.einsum("td,stc->sdc", normed_one, stacked, preferred_element_type=jnp.float32)
    d_normed_one = mp_allreduce(
        jnp.einsum("stc,sdc->td", stacked, w_qkv, preferred_element_type=jnp.float32).astype(
            jnp.bfloat16
        ),
        n_mp,
    )
    d_input_norm, grad_ln1_gain, grad_ln1_bias = norm_one_back(d_normed_one)
    grad_tokens = d_middle + d_input_norm

    def scatter(grad, dim):
        return lax.psum_scatter(
            grad.astype(jnp.bfloat16), "dp", scatter_dimension=dim, tiled=True
        ).astype(jnp.float32)

    summed_qkv = scatter(grad_w_qkv, 1)
    summed_out = scatter(grad_w_out, 1)
    summed_fc1 = scatter(grad_w_fc1, 0)
    summed_fc2 = scatter(grad_w_fc2, 1)
    packed = jnp.concatenate(
        [
            grad_ln1_gain,
            grad_ln1_bias,
            grad_ln2_gain,
            grad_ln2_bias,
            grad_b_out,
            grad_b_fc2,
            grad_b_qv.reshape(-1),
            grad_b_fc1,
        ]
    )
    packed = lax.psum(packed, "dp")
    width = grad_ln1_gain.shape[0]
    pieces = [packed[k * width : (k + 1) * width] for k in range(6)]
    qv_size = grad_b_qv.size
    summed_b_qv = packed[6 * width : 6 * width + qv_size].reshape(grad_b_qv.shape)
    summed_b_fc1 = packed[6 * width + qv_size :]
    return (
        output,
        grad_tokens,
        summed_qkv,
        summed_b_qv,
        summed_out,
        pieces[4],
        summed_fc1,
        summed_b_fc1,
        summed_fc2,
        pieces[5],
        pieces[0],
        pieces[1],
        pieces[2],
        pieces[3],
    )


def solution(mesh):
    in_specs = (
        P("dp", None),
        P("dp", None),
        P("dp", None),
        P(None, None, "mp"),
        P(None, "mp"),
        P("mp", None),
        P(),
        P(None, "mp"),
        P("mp"),
        P("mp", None),
        P(),
        P(),
        P(),
        P(),
        P(),
    )
    out_specs = (
        P("dp", None),
        P("dp", None),
        P(None, "dp", "mp"),
        P(None, "mp"),
        P("mp", "dp"),
        P(),
        P("dp", "mp"),
        P("mp"),
        P("mp", "dp"),
        P(),
        P(),
        P(),
        P(),
        P(),
    )
    return jax.shard_map(
        partial(per_device, mesh.shape["mp"]),
        mesh=mesh,
        in_specs=in_specs,
        out_specs=out_specs,
        check_vma=False,
    )
```

profile of v0, /device:TPU:0, one launch (start us, length us, event | category | flops | bytes accessed | tf_op | source)
XLA Modules:
  0.0 817.9 jit_solution(1069003523429425183)
XLA Ops:
  32.4 64.2 %while.27 = (s32[]{:T(128)}, bf16[4,512,4,64]{1,3,2,0:T(8,128)(2,1)}, f32[4,4,512]{2,1,0:T(4,128)}, s32[4,512]{1,0:T(4,128)S(1)}, s32[2048]{0:T(1024)S(1)}, /*in...) while((s32[]{:T(128)}, ...), condition=%wide.region_7.8_spmd, body=%wide.region_4.7_spmd.sunk | while | flops 1125251072 | bytes 61421712 | solution.py:110
  117.3 45.9 %collective-permute-done.1 = bf16[1024,1024]{1,0:T(8,128)(2,1)S(1)} collective-permute-done((bf16[1024,1024]{1,0:T(8,128)(2,1)S(1)}, bf16[1024,1024]{1,0:T(8,128)(2,1)S(1)}, u32[]{:S(2)}, u32[]{:S(2)}) %collective-permute-start.1) | collective-permute-done | bytes 2097184 | tf_op jit(solution)/shard_map/ppermute | solution.py:38
  184.3 25.6 %fusion.103 = (f32[1024]{0:T(1024)}, bf16[2048,1024]{1,0:T(8,128)(2,1)}, f32[2048,1024]{1,0:T(8,128)}) fusion(f32[2048,1024]{1,0:T(8,128)S(1)} %fusion.100, f32[1024]{0:T(1024)S(1)} %copy-done.54, bf16[2048,1024]{1,0:T(8,128)(2,1)S(1)} %copy-done.22, bf16[1024,1024]{1,0:T(8,128)(2,1)S(1)} %copy-done), kind=kOutput, calls=%fused_computation.182 | convolution fusion | flops 4450155520 | bytes 27271168 | tf_op jit(solution)/shard_map/td,fd->tf/dot_general | solution.py:128
  209.8 10.1 %multiply_convert_fusion.1 = bf16[2048,1024]{1,0:T(8,128)(2,1)} fusion(f32[2048,1024]{1,0:T(8,128)} %get-tuple-element.335, f32[2048,1024]{1,0:T(8,128)} %copy-done.21, f32[1024]{0:T(1024)S(1)} %copy-done.54), kind=kLoop, calls=%fused_computation.86 | loop fusion | flops 8388608 | bytes 20975616 | tf_op jit(solution)/shard_map/convert_element_type | solution.py:120
  256.8 43.6 %collective-permute-done.7 = bf16[1024,1024]{1,0:T(8,128)(2,1)S(1)} collective-permute-done((bf16[1024,1024]{1,0:T(8,128)(2,1)S(1)}, bf16[1024,1024]{1,0:T(8,128)(2,1)S(1)}, u32[]{:S(2)}, u32[]{:S(2)}) %collective-permute-start.7) | collective-permute-done | bytes 2097184 | tf_op jit(solution)/shard_map/ppermute | solution.py:38
  302.7 11.1 %fusion.77 = bf16[1024,1024]{1,0:T(8,128)(2,1)} fusion(bf16[2048,1024]{1,0:T(8,128)(2,1)} %get-tuple-element.334, f32[1024]{0:T(1024)S(1)} %copy-done.57, f32[1024]{0:T(1024)S(1)} %copy-done.46, f32[2048]{0:T(1024)S(1)} %fusion.96, bf16[2048,1024]{1,0:T(8,128)(2,1)} %param.19, f32[2048]{0:T(1024)S(1)} %broadcast_multiply_fusion, f32[1024]{0:T(1024)S(1)} %copy-done.38, ...), kind=kOutput, calls=%fused_computation.142 | convolution fusion | flops 4321181696 | bytes 14708736 | tf_op jit(solution)/shard_map/td,tf->df/dot_general | solution.py:132
  314.0 30.5 %collective-permute-done.4 = bf16[1024,1024]{1,0:T(8,128)(2,1)} collective-permute-done((bf16[1024,1024]{1,0:T(8,128)(2,1)}, bf16[1024,1024]{1,0:T(8,128)(2,1)}, u32[]{:S(2)}, u32[]{:S(2)}) %collective-permute-start.4) | collective-permute-done | bytes 2097184 | tf_op jit(solution)/shard_map/ppermute | solution.py:38
  356.9 9.5 %fusion.57 = (f32[1024]{0:T(1024)}, f32[2048]{0:T(1024)S(1)}, f32[1024]{0:T(1024)}) fusion(f32[2048]{0:T(1024)S(1)} %fusion.96, bf16[1024,1024]{1,0:T(8,128)(2,1)S(1)} %get-tuple-element.347, bf16[1024,1024]{1,0:T(8,128)(2,1)S(1)} %get-tuple-element.346, f32[2048]{0:T(1024)S(1)} %broadcast_multiply_fusion, f32[1024]{0:T(1024)S(1)} %copy-done.38, ...), kind=kLoop, calls=%fused_computation.80 | loop fusion | flops 46133248 | bytes 12632064 | tf_op jit(solution)/shard_map/transpose(jvp())/reduce_sum | solution.py:15
  366.8 11.7 %fusion.105 = (f32[1024]{0:T(1024)}, f32[2048,1024]{1,0:T(8,128)S(1)}, bf16[2048,1024]{1,0:T(8,128)(2,1)}, f32[1024]{0:T(1024)}) fusion(f32[2048]{0:T(1024)S(1)} %negate_multiply_fusion.2, f32[2048]{0:T(1024)S(1)} %multiply_multiply_fusion.6, f32[2048]{0:T(1024)S(1)} %broadcast_multiply_fusion, f32[1024]{0:T(1024)S(1)} %copy-done.38, ...), kind=kLoop, calls=%fused_computation.183 | loop fusion | flops 60815360 | bytes 33607680 | tf_op jit(solution)/shard_map/reduce_sum | solution.py:141
  389.9 195.7 %while.28 = (s32[]{:T(128)}, f32[2048,4,64]{0,2,1:T(8,128)}, f32[2048,4,64]{0,2,1:T(8,128)}, f32[4,512,4,64]{1,3,2,0:T(8,128)}, bf16[4,512,4,64]{1,3,2,0:T(8,128...) while((s32[]{:T(128)}, f32[2048,4,64]{0,2,1:T(8,128)}, ...), condition=%wide.region_14.15_spmd.clone, body=%wide.region_12.14_spmd.clone.sunk | while | flops 2751068160 | bytes 164206880 | solution.py:179
  403.0 11.5 %multiply_reduce_fusion.3 = (f32[4,512]{1,0:T(4,128)}, f32[4,512,2048]{2,1,0:T(8,128)}) fusion(f32[4,512,2048]{2,1,0:T(8,128)S(1)} %fusion.167, f32[4,512]{1,0:T(4,128)S(1)} %dynamic-slice_bitcast_fusion.2, pred[512,2048]{1,0:T(8,128)(4,1)} %copy-done.8, bf16[2048,4,64]{0,2,1:T(8,128)(2,1)} %get-tuple-element.555, ...), kind=kOutput, calls=%fused_computation.19.clone.1 | convolution fusion | flops 557840384 | bytes 35930116 | tf_op jit(solution)/shard_map/while/body/eval_jaxpr/qhd,khd->hqk/dot_general | solution.py:154
  414.5 11.1 %multiply_convert_fusion.3 = bf16[4,512,2048]{2,1,0:T(8,128)(2,1)} fusion(f32[4,512,2048]{2,1,0:T(8,128)} %get-tuple-element.490, f32[4,512,2048]{2,1,0:T(8,128)S(1)} %fusion.167, f32[4,512]{1,0:T(4,128)} %get-tuple-element.491, f32[4,512]{1,0:T(4,128)S(1)} %dynamic-slice_bitcast_fusion.2, pred[512,2048]{1,0:T(8,128)(4,1)} %copy-done.8), kind=kLoop, calls=%fused_computation.18.clone.1 | loop fusion | flops 25165824 | bytes 43008000 | tf_op jit(solution)/shard_map/while/body/eval_jaxpr/convert_element_type | solution.py:158
  451.9 11.5 %multiply_reduce_fusion.3 = (f32[4,512]{1,0:T(4,128)}, f32[4,512,2048]{2,1,0:T(8,128)}) fusion(f32[4,512,2048]{2,1,0:T(8,128)S(1)} %fusion.167, f32[4,512]{1,0:T(4,128)S(1)} %dynamic-slice_bitcast_fusion.2, pred[512,2048]{1,0:T(8,128)(4,1)} %copy-done.8, bf16[2048,4,64]{0,2,1:T(8,128)(2,1)} %get-tuple-element.555, ...), kind=kOutput, calls=%fused_computation.19.clone.1 | convolution fusion | flops 557840384 | bytes 35930116 | tf_op jit(solution)/shard_map/while/body/eval_jaxpr/qhd,khd->hqk/dot_general | solution.py:154
  463.4 11.1 %multiply_convert_fusion.3 = bf16[4,512,2048]{2,1,0:T(8,128)(2,1)} fusion(f32[4,512,2048]{2,1,0:T(8,128)} %get-tuple-element.490, f32[4,512,2048]{2,1,0:T(8,128)S(1)} %fusion.167, f32[4,512]{1,0:T(4,128)} %get-tuple-element.491, f32[4,512]{1,0:T(4,128)S(1)} %dynamic-slice_bitcast_fusion.2, pred[512,2048]{1,0:T(8,128)(4,1)} %copy-done.8), kind=kLoop, calls=%fused_computation.18.clone.1 | loop fusion | flops 25165824 | bytes 43008000 | tf_op jit(solution)/shard_map/while/body/eval_jaxpr/convert_element_type | solution.py:158
  500.8 11.5 %multiply_reduce_fusion.3 = (f32[4,512]{1,0:T(4,128)}, f32[4,512,2048]{2,1,0:T(8,128)}) fusion(f32[4,512,2048]{2,1,0:T(8,128)S(1)} %fusion.167, f32[4,512]{1,0:T(4,128)S(1)} %dynamic-slice_bitcast_fusion.2, pred[512,2048]{1,0:T(8,128)(4,1)} %copy-done.8, bf16[2048,4,64]{0,2,1:T(8,128)(2,1)} %get-tuple-element.555, ...), kind=kOutput, calls=%fused_computation.19.clone.1 | convolution fusion | flops 557840384 | bytes 35930116 | tf_op jit(solution)/shard_map/while/body/eval_jaxpr/qhd,khd->hqk/dot_general | solution.py:154
  512.3 11.1 %multiply_convert_fusion.3 = bf16[4,512,2048]{2,1,0:T(8,128)(2,1)} fusion(f32[4,512,2048]{2,1,0:T(8,128)} %get-tuple-element.490, f32[4,512,2048]{2,1,0:T(8,128)S(1)} %fusion.167, f32[4,512]{1,0:T(4,128)} %get-tuple-element.491, f32[4,512]{1,0:T(4,128)S(1)} %dynamic-slice_bitcast_fusion.2, pred[512,2048]{1,0:T(8,128)(4,1)} %copy-done.8), kind=kLoop, calls=%fused_computation.18.clone.1 | loop fusion | flops 25165824 | bytes 43008000 | tf_op jit(solution)/shard_map/while/body/eval_jaxpr/convert_element_type | solution.py:158
  549.7 11.5 %multiply_reduce_fusion.3 = (f32[4,512]{1,0:T(4,128)}, f32[4,512,2048]{2,1,0:T(8,128)}) fusion(f32[4,512,2048]{2,1,0:T(8,128)S(1)} %fusion.167, f32[4,512]{1,0:T(4,128)S(1)} %dynamic-slice_bitcast_fusion.2, pred[512,2048]{1,0:T(8,128)(4,1)} %copy-done.8, bf16[2048,4,64]{0,2,1:T(8,128)(2,1)} %get-tuple-element.555, ...), kind=kOutput, calls=%fused_computation.19.clone.1 | convolution fusion | flops 557840384 | bytes 35930116 | tf_op jit(solution)/shard_map/while/body/eval_jaxpr/qhd,khd->hqk/dot_general | solution.py:154
  561.1 11.1 %multiply_convert_fusion.3 = bf16[4,512,2048]{2,1,0:T(8,128)(2,1)} fusion(f32[4,512,2048]{2,1,0:T(8,128)} %get-tuple-element.490, f32[4,512,2048]{2,1,0:T(8,128)S(1)} %fusion.167, f32[4,512]{1,0:T(4,128)} %get-tuple-element.491, f32[4,512]{1,0:T(4,128)S(1)} %dynamic-slice_bitcast_fusion.2, pred[512,2048]{1,0:T(8,128)(4,1)} %copy-done.8), kind=kLoop, calls=%fused_computation.18.clone.1 | loop fusion | flops 25165824 | bytes 43008000 | tf_op jit(solution)/shard_map/while/body/eval_jaxpr/convert_element_type | solution.py:158
  616.6 7.9 fusion.83
  632.0 25.2 %collective-permute-done.10 = bf16[1024,1024]{1,0:T(8,128)(2,1)} collective-permute-done((bf16[1024,1024]{1,0:T(8,128)(2,1)S(1)}, bf16[1024,1024]{1,0:T(8,128)(2,1)}, u32[]{:S(2)}, u32[]{:S(2)}) %collective-permute-start.10) | collective-permute-done | bytes 2097184 | tf_op jit(solution)/shard_map/ppermute | solution.py:38
  665.0 14.6 %reduce-scatter.15.cloned.1.call-done = bf16[128,256]{1,0:T(8,128)(2,1)} async-done(((bf16[1024,256]{1,0:T(8,128)(2,1)}), bf16[128,256]{1,0:T(8,128)(2,1)}) %reduce-scatter.15.cloned.1.call-update) | async-done | bytes 65552
  681.3 66.3 %reduce-scatter.13.cloned.1.call-done = bf16[128,768]{1,0:T(8,128)(2,1)} async-done(((bf16[1024,768]{1,0:T(8,128)(2,1)}), bf16[128,768]{1,0:T(8,128)(2,1)}) %reduce-scatter.13.cloned.1.call-update) | async-done | bytes 196624
  763.0 34.7 %psum.7 = f32[7680]{0:T(1024)S(1)} all-reduce(f32[7680]{0:T(1024)S(1)} %constant_dynamic-update-slice_fusion), channel_id=1, replica_groups=mesh['dp'=8,'mp'=4] {'dp'}, use_global_device_ids=true, to_apply=%region_27.28 | all-reduce | flops 7680 | bytes 61440 | tf_op jit(solution)/shard_map/psum | solution.py:218
  798.3 12.3 %add_add_fusion.2 = f32[2048,1024]{1,0:T(8,128)} fusion(f32[2048,1024]{1,0:T(8,128)} %copy-done.9, bf16[2048,1024]{1,0:T(8,128)(2,1)} %param.19, f32[2048]{0:T(1024)S(1)} %negate_multiply_fusion.1, f32[2048]{0:T(1024)S(1)} %multiply_multiply_fusion.5, f32[1024]{0:T(1024)S(1)} %copy-done.45, f32[2048]{0:T(1024)S(1)} %copy-done.37, f32[2048]{0:T(1024)S(1)} %copy-done.35, ...), kind=kLoop, calls=%fused_computation.83 | loop fusion | flops 27262976 | bytes 25202688 | tf_op jit(solution)/shard_map/add | solution.py:195
  (320 shorter events, 362.5 us)
Async XLA Ops:
  7.2 177.0 %copy-start = (bf16[1024,1024]{1,0:T(8,128)(2,1)S(1)}, bf16[1024,1024]{1,0:T(8,128)(2,1)}, u32[]{:S(2)}) copy-start(bf16[1024,1024]{1,0:T(8,128)(2,1)} %param.28) | copy-start | bytes 6291460
  7.2 653.9 %reduce-scatter.17.cloned.1.call-start = ((), (), s32[]{:S(2)}) async-start(), calls=%async_computation.7 | async-start | bytes 2359296
  106.5 4.7 collective-permute-start
  114.4 58.2 %copy-start.38 = (f32[1024]{0:T(1024)S(1)}, f32[1024]{0:T(1024)}, u32[]{:S(2)}) copy-start(f32[1024]{0:T(1024)} %param.25) | copy-start | bytes 12292
  114.4 48.9 %collective-permute-start.1 = (bf16[1024,1024]{1,0:T(8,128)(2,1)S(1)}, bf16[1024,1024]{1,0:T(8,128)(2,1)S(1)}, u32[]{:S(2)}, u32[]{:S(2)}) collective-permute-start(bf16[1024,1024]{1,0:T(8,128)(2,1)S(1)} %add_convert_fusion.9), channel_id=1, source_target_pairs={{0,2},{1,3},{2,0},{3,1},{4,6},{5,7},{6,4},{7,5},{8,10},{9,11},{10,... | collective-permute-start | bytes 6291464 | tf_op jit(solution)/shard_map/ppermute | solution.py:38
  165.5 4.5 collective-permute-start.2
  184.3 25.6 %copy-start.21 = (f32[2048,1024]{1,0:T(8,128)}, f32[2048,1024]{1,0:T(8,128)S(1)}, u32[]{:S(2)}) copy-start(f32[2048,1024]{1,0:T(8,128)S(1)} %fusion.100) | copy-start | bytes 25165828
  230.6 18.3 %collective-permute-start.6 = (bf16[1024,1024]{1,0:T(8,128)(2,1)}, bf16[1024,1024]{1,0:T(8,128)(2,1)}, u32[]{:S(2)}, u32[]{:S(2)}) collective-permute-start(bf16[1024,1024]{1,0:T(8,128)(2,1)} %constant_dynamic-slice_fusion.3), channel_id=1, source_target_pairs={{0,1},{1,0},{2,3},{3,2},{4,5},{5,4},{6,7},{7,6},{8,9},{9,8},{10,11... | collective-permute-start | bytes 6291464 | tf_op jit(solution)/shard_map/ppermute | solution.py:36
  240.6 422.5 %reduce-scatter.11.cloned.1.call-start = ((), (), s32[]{:S(2)}) async-start(), calls=%async_computation.4 | async-start | bytes 2359296 | tf_op jit(solution)/shard_map/reduce_scatter | solution.py:198
  248.5 54.2 %copy-start.13 = (bf16[1024,1024]{1,0:T(8,128)(2,1)S(1)}, bf16[1024,1024]{1,0:T(8,128)(2,1)}, u32[]{:S(2)}) copy-start(bf16[1024,1024]{1,0:T(8,128)(2,1)} %copy-done.12) | copy-start | bytes 6291460
  248.5 5.2 collective-permute-start.3
  251.9 48.6 %collective-permute-start.7 = (bf16[1024,1024]{1,0:T(8,128)(2,1)S(1)}, bf16[1024,1024]{1,0:T(8,128)(2,1)S(1)}, u32[]{:S(2)}, u32[]{:S(2)}) collective-permute-start(bf16[1024,1024]{1,0:T(8,128)(2,1)S(1)} %add_convert_fusion.5), channel_id=1, source_target_pairs={{0,2},{1,3},{2,0},{3,1},{4,6},{5,7},{6,4},{7,5},{8,10},{9,11},{10,... | collective-permute-start | bytes 6291464 | tf_op jit(solution)/shard_map/ppermute | solution.py:38
  256.0 88.6 %collective-permute-start.4 = (bf16[1024,1024]{1,0:T(8,128)(2,1)}, bf16[1024,1024]{1,0:T(8,128)(2,1)}, u32[]{:S(2)}, u32[]{:S(2)}) collective-permute-start(bf16[1024,1024]{1,0:T(8,128)(2,1)} %add_convert_fusion.7), channel_id=1, source_target_pairs={{0,2},{1,3},{2,0},{3,1},{4,6},{5,7},{6,4},{7,5},{8,10},{9,11},{10,... | collective-permute-start | bytes 6291464 | tf_op jit(solution)/shard_map/ppermute | solution.py:38
  302.7 45.2 %collective-permute-start.8 = (bf16[1024,1024]{1,0:T(8,128)(2,1)}, bf16[1024,1024]{1,0:T(8,128)(2,1)}, u32[]{:S(2)}, u32[]{:S(2)}) collective-permute-start(bf16[1024,1024]{1,0:T(8,128)(2,1)} %add_convert_fusion.4), channel_id=1, source_target_pairs={{0,1},{1,0},{2,3},{3,2},{4,5},{5,4},{6,7},{7,6},{8,9},{9,8},{10,11... | collective-permute-start | bytes 6291464 | tf_op jit(solution)/shard_map/ppermute | solution.py:40
  313.8 365.8 %reduce-scatter.15.cloned.1.call-start = ((), (), s32[]{:S(2)}) async-start(), calls=%async_computation.6 | async-start | bytes 589824
  314.0 36.5 %copy-start.4 = (bf16[2048,1024]{1,0:T(8,128)(2,1)S(1)}, bf16[2048,1024]{1,0:T(8,128)(2,1)}, u32[]{:S(2)}) copy-start(bf16[2048,1024]{1,0:T(8,128)(2,1)} %param.19) | copy-start | bytes 12582916
  314.0 36.5 %copy-start.15 = (bf16[1024,1024]{1,0:T(8,128)(2,1)S(1)}, bf16[1024,1024]{1,0:T(8,128)(2,1)}, u32[]{:S(2)}) copy-start(bf16[1024,1024]{1,0:T(8,128)(2,1)} %copy-done.14) | copy-start | bytes 6291460
  347.8 18.7 %collective-permute-start.5 = (bf16[1024,1024]{1,0:T(8,128)(2,1)S(1)}, bf16[1024,1024]{1,0:T(8,128)(2,1)S(1)}, u32[]{:S(2)}, u32[]{:S(2)}) collective-permute-start(bf16[1024,1024]{1,0:T(8,128)(2,1)S(1)} %add_convert_fusion.6), channel_id=1, source_target_pairs={{0,1},{1,0},{2,3},{3,2},{4,5},{5,4},{6,7},{7,6},{8,9},{9,8},{10,11... | collective-permute-start | bytes 6291464 | tf_op jit(solution)/shard_map/ppermute | solution.py:40
  603.8 4.3 collective-permute-start.9
  609.1 48.1 %collective-permute-start.10 = (bf16[1024,1024]{1,0:T(8,128)(2,1)S(1)}, bf16[1024,1024]{1,0:T(8,128)(2,1)}, u32[]{:S(2)}, u32[]{:S(2)}) collective-permute-start(bf16[1024,1024]{1,0:T(8,128)(2,1)S(1)} %add_convert_fusion.3), channel_id=1, source_target_pairs={{0,2},{1,3},{2,0},{3,1},{4,6},{5,7},{6,4},{7,5},{8,10},{9,11},{10,... | collective-permute-start | bytes 6291464 | tf_op jit(solution)/shard_map/ppermute | solution.py:38
  616.6 131.0 %reduce-scatter.13.cloned.1.call-start = ((), (), s32[]{:S(2)}) async-start(), calls=%async_computation.5 | async-start | bytes 1769472
  632.0 119.7 %copy-start.35 = (f32[2048]{0:T(1024)S(1)}, f32[2048]{0:T(1024)}, u32[]{:S(2)}) copy-start(f32[2048]{0:T(1024)} %copy-done.34) | copy-start | bytes 24580
  632.0 119.7 %copy-start.45 = (f32[1024]{0:T(1024)S(1)}, f32[1024]{0:T(1024)}, u32[]{:S(2)}) copy-start(f32[1024]{0:T(1024)} %param.30) | copy-start | bytes 12292
  661.1 88.6 %collective-permute-start.11 = (bf16[1024,1024]{1,0:T(8,128)(2,1)}, bf16[1024,1024]{1,0:T(8,128)(2,1)S(1)}, u32[]{:S(2)}, u32[]{:S(2)}) collective-permute-start(bf16[1024,1024]{1,0:T(8,128)(2,1)} %add_convert_fusion.2), channel_id=1, source_target_pairs={{0,1},{1,0},{2,3},{3,2},{4,5},{5,4},{6,7},{7,6},{8,9},{9,8},{10,11... | collective-permute-start | bytes 6291464 | tf_op jit(solution)/shard_map/ppermute | solution.py:40
  (65 other events, 488.7 us)
Sparse Core Ops, SparseCore 0:
  240.7 69.8 reduce-scatter.16
  314.1 69.8 reduce-scatter.10
  616.7 62.8 reduce-scatter.14
  682.9 64.5 reduce-scatter.12
where the time goes:
time: 828 us; the launch traced here: 818 us
  matrix products  276 us (33%)
  waiting for transfers between devices  239 us (29%)
  other arithmetic  182 us (22%)
  local copies, waits for them, and re-layouts  61.1 us (7%)
  blocking collectives  34.7 us (4%)
  between operations  14.9 us (2%)
  starting transfers between devices  9.39 us (1%)
    ppermute x4, waiting for transfers between devices, mp_allreduce(): got_far = lax.ppermute(first, 'mp', [(k, k ^ 2) for k in range(4)])  145 us
    unnamed x7, waiting for transfers between devices  81 us
    dot_general x4, matrix products, backward_block(): jnp.einsum('qhd,khd->hqk', d_out_block, value_heads, preferred_element_ty...  46 us
    convert_element_type x4, other arithmetic, backward_block(): d_scores_low = d_scores.astype(jnp.bfloat16)  44.5 us
    psum x1, blocking collectives, per_device(): packed = lax.psum(packed, 'dp')  34.7 us
    dot_general x8, matrix products, block_scores(): jnp.einsum('qhd,khd->hqk', query_block, key_heads, preferred_element_type...  31.8 us
    dot_general x4, matrix products, backward_block(): jnp.einsum('hqk,khd->qhd', d_scores_low, key_heads, preferred_element_typ...  30.6 us
    unnamed x125, local copies, waits for them, and re-layouts  30.4 us
  transfers between devices with their start and end apart: 16, of which 9 were waited for; matrix products, arithmetic and copies ran while one was open for 40% of the time, Pallas kernels for 0%

commit v1 on v0

--- a/solution.py
+++ b/solution.py
@@ -215,7 +215,7 @@
             grad_b_fc1,
         ]
     )
-    packed = lax.psum(packed, "dp")
+    packed = jnp.sum(lax.all_gather(packed, "dp"), axis=0)
     width = grad_ln1_gain.shape[0]
     pieces = [packed[k * width : (k + 1) * width] for k in range(6)]
     qv_size = grad_b_qv.size

time: 828 us -> 825 us (level)
    psum x1 -> x0, blocking collectives: 34.7 us -> none  [per_device(): packed = lax.psum(packed, 'dp')]
    all_gather x0 -> x1, blocking collectives: none -> 30.7 us  [per_device(): packed = jnp.sum(lax.all_gather(packed, 'dp'), axis=0)]
    unnamed x125 -> x126, local copies, waits for them, and re-layouts: 30.4 us -> 30.4 us
where the time goes in v1:
time: 825 us; the launch traced here: 814 us
  matrix products  276 us (33%)
  waiting for transfers between devices  239 us (29%)
  other arithmetic  182 us (22%)
  local copies, waits for them, and re-layouts  61.2 us (7%)
  blocking collectives  30.7 us (4%)
  between operations  15 us (2%)
  starting transfers between devices  9.39 us (1%)
    ppermute x4, waiting for transfers between devices, mp_allreduce(): got_far = lax.ppermute(first, 'mp', [(k, k ^ 2) for k in range(4)])  145 us
    unnamed x7, waiting for transfers between devices  81 us
    dot_general x4, matrix products, backward_block(): jnp.einsum('qhd,khd->hqk', d_out_block, value_heads, preferred_element_ty...  46 us
    convert_element_type x4, other arithmetic, backward_block(): d_scores_low = d_scores.astype(jnp.bfloat16)  44.5 us
    dot_general x8, matrix products, block_scores(): jnp.einsum('qhd,khd->hqk', query_block, key_heads, preferred_element_type...  31.8 us
    all_gather x1, blocking collectives, per_device(): packed = jnp.sum(lax.all_gather(packed, 'dp'), axis=0)  30.7 us
    dot_general x4, matrix products, backward_block(): jnp.einsum('hqk,khd->qhd', d_scores_low, key_heads, preferred_element_typ...  30.6 us
    unnamed x126, local copies, waits for them, and re-layouts  30.4 us
  transfers between devices with their start and end apart: 16, of which 9 were waited for; matrix products, arithmetic and copies ran while one was open for 40% of the time, Pallas kernels for 0%

profile of v1, /device:TPU:0, one launch (start us, length us, event | category | flops | bytes accessed | tf_op | source)
XLA Modules:
  0.0 814.2 jit_solution(3464498612069114334)
XLA Ops:
  32.4 64.2 %while.27 = (s32[]{:T(128)}, bf16[4,512,4,64]{1,3,2,0:T(8,128)(2,1)}, f32[4,4,512]{2,1,0:T(4,128)}, s32[4,512]{1,0:T(4,128)S(1)}, s32[2048]{0:T(1024)S(1)}, /*in...) while((s32[]{:T(128)}, ...), condition=%wide.region_7.8_spmd, body=%wide.region_4.7_spmd.sunk | while | flops 1125251072 | bytes 61421712 | solution.py:110
  117.3 45.9 %collective-permute-done.1 = bf16[1024,1024]{1,0:T(8,128)(2,1)S(1)} collective-permute-done((bf16[1024,1024]{1,0:T(8,128)(2,1)S(1)}, bf16[1024,1024]{1,0:T(8,128)(2,1)S(1)}, u32[]{:S(2)}, u32[]{:S(2)}) %collective-permute-start.1) | collective-permute-done | bytes 2097184 | tf_op jit(solution)/shard_map/ppermute | solution.py:38
  184.3 25.6 %fusion.103 = (f32[1024]{0:T(1024)}, bf16[2048,1024]{1,0:T(8,128)(2,1)}, f32[2048,1024]{1,0:T(8,128)}) fusion(f32[2048,1024]{1,0:T(8,128)S(1)} %fusion.100, f32[1024]{0:T(1024)S(1)} %copy-done.54, bf16[2048,1024]{1,0:T(8,128)(2,1)S(1)} %copy-done.22, bf16[1024,1024]{1,0:T(8,128)(2,1)S(1)} %copy-done), kind=kOutput, calls=%fused_computation.182 | convolution fusion | flops 4450155520 | bytes 27271168 | tf_op jit(solution)/shard_map/td,fd->tf/dot_general | solution.py:128
  209.8 10.1 %multiply_convert_fusion.1 = bf16[2048,1024]{1,0:T(8,128)(2,1)} fusion(f32[2048,1024]{1,0:T(8,128)} %get-tuple-element.335, f32[2048,1024]{1,0:T(8,128)} %copy-done.21, f32[1024]{0:T(1024)S(1)} %copy-done.54), kind=kLoop, calls=%fused_computation.86 | loop fusion | flops 8388608 | bytes 20975616 | tf_op jit(solution)/shard_map/convert_element_type | solution.py:120
  256.8 43.6 %collective-permute-done.7 = bf16[1024,1024]{1,0:T(8,128)(2,1)S(1)} collective-permute-done((bf16[1024,1024]{1,0:T(8,128)(2,1)S(1)}, bf16[1024,1024]{1,0:T(8,128)(2,1)S(1)}, u32[]{:S(2)}, u32[]{:S(2)}) %collective-permute-start.7) | collective-permute-done | bytes 2097184 | tf_op jit(solution)/shard_map/ppermute | solution.py:38
  302.7 11.1 %fusion.77 = bf16[1024,1024]{1,0:T(8,128)(2,1)} fusion(bf16[2048,1024]{1,0:T(8,128)(2,1)} %get-tuple-element.334, f32[1024]{0:T(1024)S(1)} %copy-done.57, f32[1024]{0:T(1024)S(1)} %copy-done.46, f32[2048]{0:T(1024)S(1)} %fusion.96, bf16[2048,1024]{1,0:T(8,128)(2,1)} %param.19, f32[2048]{0:T(1024)S(1)} %broadcast_multiply_fusion, f32[1024]{0:T(1024)S(1)} %copy-done.38, ...), kind=kOutput, calls=%fused_computation.142 | convolution fusion | flops 4321181696 | bytes 14708736 | tf_op jit(solution)/shard_map/td,tf->df/dot_general | solution.py:132
  314.0 30.5 %collective-permute-done.4 = bf16[1024,1024]{1,0:T(8,128)(2,1)} collective-permute-done((bf16[1024,1024]{1,0:T(8,128)(2,1)}, bf16[1024,1024]{1,0:T(8,128)(2,1)}, u32[]{:S(2)}, u32[]{:S(2)}) %collective-permute-start.4) | collective-permute-done | bytes 2097184 | tf_op jit(solution)/shard_map/ppermute | solution.py:38
  356.9 9.5 %fusion.57 = (f32[1024]{0:T(1024)}, f32[2048]{0:T(1024)S(1)}, f32[1024]{0:T(1024)}) fusion(f32[2048]{0:T(1024)S(1)} %fusion.96, bf16[1024,1024]{1,0:T(8,128)(2,1)S(1)} %get-tuple-element.347, bf16[1024,1024]{1,0:T(8,128)(2,1)S(1)} %get-tuple-element.346, f32[2048]{0:T(1024)S(1)} %broadcast_multiply_fusion, f32[1024]{0:T(1024)S(1)} %copy-done.38, ...), kind=kLoop, calls=%fused_computation.80 | loop fusion | flops 46133248 | bytes 12632064 | tf_op jit(solution)/shard_map/transpose(jvp())/reduce_sum | solution.py:15
  366.8 11.7 %fusion.105 = (f32[1024]{0:T(1024)}, f32[2048,1024]{1,0:T(8,128)S(1)}, bf16[2048,1024]{1,0:T(8,128)(2,1)}, f32[1024]{0:T(1024)}) fusion(f32[2048]{0:T(1024)S(1)} %negate_multiply_fusion.2, f32[2048]{0:T(1024)S(1)} %multiply_multiply_fusion.6, f32[2048]{0:T(1024)S(1)} %broadcast_multiply_fusion, f32[1024]{0:T(1024)S(1)} %copy-done.38, ...), kind=kLoop, calls=%fused_computation.183 | loop fusion | flops 60815360 | bytes 33607680 | tf_op jit(solution)/shard_map/reduce_sum | solution.py:141
  389.9 195.7 %while.28 = (s32[]{:T(128)}, f32[2048,4,64]{0,2,1:T(8,128)}, f32[2048,4,64]{0,2,1:T(8,128)}, f32[4,512,4,64]{1,3,2,0:T(8,128)}, bf16[4,512,4,64]{1,3,2,0:T(8,128...) while((s32[]{:T(128)}, f32[2048,4,64]{0,2,1:T(8,128)}, ...), condition=%wide.region_14.15_spmd.clone, body=%wide.region_12.14_spmd.clone.sunk | while | flops 2751068160 | bytes 164206880 | solution.py:179
  403.0 11.5 %multiply_reduce_fusion.3 = (f32[4,512]{1,0:T(4,128)}, f32[4,512,2048]{2,1,0:T(8,128)}) fusion(f32[4,512,2048]{2,1,0:T(8,128)S(1)} %fusion.167, f32[4,512]{1,0:T(4,128)S(1)} %dynamic-slice_bitcast_fusion.2, pred[512,2048]{1,0:T(8,128)(4,1)} %copy-done.8, bf16[2048,4,64]{0,2,1:T(8,128)(2,1)} %get-tuple-element.555, ...), kind=kOutput, calls=%fused_computation.19.clone.1 | convolution fusion | flops 557840384 | bytes 35930116 | tf_op jit(solution)/shard_map/while/body/eval_jaxpr/qhd,khd->hqk/dot_general | solution.py:154
  414.5 11.1 %multiply_convert_fusion.3 = bf16[4,512,2048]{2,1,0:T(8,128)(2,1)} fusion(f32[4,512,2048]{2,1,0:T(8,128)} %get-tuple-element.490, f32[4,512,2048]{2,1,0:T(8,128)S(1)} %fusion.167, f32[4,512]{1,0:T(4,128)} %get-tuple-element.491, f32[4,512]{1,0:T(4,128)S(1)} %dynamic-slice_bitcast_fusion.2, pred[512,2048]{1,0:T(8,128)(4,1)} %copy-done.8), kind=kLoop, calls=%fused_computation.18.clone.1 | loop fusion | flops 25165824 | bytes 43008000 | tf_op jit(solution)/shard_map/while/body/eval_jaxpr/convert_element_type | solution.py:158
  451.9 11.5 %multiply_reduce_fusion.3 = (f32[4,512]{1,0:T(4,128)}, f32[4,512,2048]{2,1,0:T(8,128)}) fusion(f32[4,512,2048]{2,1,0:T(8,128)S(1)} %fusion.167, f32[4,512]{1,0:T(4,128)S(1)} %dynamic-slice_bitcast_fusion.2, pred[512,2048]{1,0:T(8,128)(4,1)} %copy-done.8, bf16[2048,4,64]{0,2,1:T(8,128)(2,1)} %get-tuple-element.555, ...), kind=kOutput, calls=%fused_computation.19.clone.1 | convolution fusion | flops 557840384 | bytes 35930116 | tf_op jit(solution)/shard_map/while/body/eval_jaxpr/qhd,khd->hqk/dot_general | solution.py:154
  463.4 11.1 %multiply_convert_fusion.3 = bf16[4,512,2048]{2,1,0:T(8,128)(2,1)} fusion(f32[4,512,2048]{2,1,0:T(8,128)} %get-tuple-element.490, f32[4,512,2048]{2,1,0:T(8,128)S(1)} %fusion.167, f32[4,512]{1,0:T(4,128)} %get-tuple-element.491, f32[4,512]{1,0:T(4,128)S(1)} %dynamic-slice_bitcast_fusion.2, pred[512,2048]{1,0:T(8,128)(4,1)} %copy-done.8), kind=kLoop, calls=%fused_computation.18.clone.1 | loop fusion | flops 25165824 | bytes 43008000 | tf_op jit(solution)/shard_map/while/body/eval_jaxpr/convert_element_type | solution.py:158
  500.8 11.5 %multiply_reduce_fusion.3 = (f32[4,512]{1,0:T(4,128)}, f32[4,512,2048]{2,1,0:T(8,128)}) fusion(f32[4,512,2048]{2,1,0:T(8,128)S(1)} %fusion.167, f32[4,512]{1,0:T(4,128)S(1)} %dynamic-slice_bitcast_fusion.2, pred[512,2048]{1,0:T(8,128)(4,1)} %copy-done.8, bf16[2048,4,64]{0,2,1:T(8,128)(2,1)} %get-tuple-element.555, ...), kind=kOutput, calls=%fused_computation.19.clone.1 | convolution fusion | flops 557840384 | bytes 35930116 | tf_op jit(solution)/shard_map/while/body/eval_jaxpr/qhd,khd->hqk/dot_general | solution.py:154
  512.3 11.1 %multiply_convert_fusion.3 = bf16[4,512,2048]{2,1,0:T(8,128)(2,1)} fusion(f32[4,512,2048]{2,1,0:T(8,128)} %get-tuple-element.490, f32[4,512,2048]{2,1,0:T(8,128)S(1)} %fusion.167, f32[4,512]{1,0:T(4,128)} %get-tuple-element.491, f32[4,512]{1,0:T(4,128)S(1)} %dynamic-slice_bitcast_fusion.2, pred[512,2048]{1,0:T(8,128)(4,1)} %copy-done.8), kind=kLoop, calls=%fused_computation.18.clone.1 | loop fusion | flops 25165824 | bytes 43008000 | tf_op jit(solution)/shard_map/while/body/eval_jaxpr/convert_element_type | solution.py:158
  549.7 11.5 %multiply_reduce_fusion.3 = (f32[4,512]{1,0:T(4,128)}, f32[4,512,2048]{2,1,0:T(8,128)}) fusion(f32[4,512,2048]{2,1,0:T(8,128)S(1)} %fusion.167, f32[4,512]{1,0:T(4,128)S(1)} %dynamic-slice_bitcast_fusion.2, pred[512,2048]{1,0:T(8,128)(4,1)} %copy-done.8, bf16[2048,4,64]{0,2,1:T(8,128)(2,1)} %get-tuple-element.555, ...), kind=kOutput, calls=%fused_computation.19.clone.1 | convolution fusion | flops 557840384 | bytes 35930116 | tf_op jit(solution)/shard_map/while/body/eval_jaxpr/qhd,khd->hqk/dot_general | solution.py:154
  561.1 11.1 %multiply_convert_fusion.3 = bf16[4,512,2048]{2,1,0:T(8,128)(2,1)} fusion(f32[4,512,2048]{2,1,0:T(8,128)} %get-tuple-element.490, f32[4,512,2048]{2,1,0:T(8,128)S(1)} %fusion.167, f32[4,512]{1,0:T(4,128)} %get-tuple-element.491, f32[4,512]{1,0:T(4,128)S(1)} %dynamic-slice_bitcast_fusion.2, pred[512,2048]{1,0:T(8,128)(4,1)} %copy-done.8), kind=kLoop, calls=%fused_computation.18.clone.1 | loop fusion | flops 25165824 | bytes 43008000 | tf_op jit(solution)/shard_map/while/body/eval_jaxpr/convert_element_type | solution.py:158
  616.6 7.9 fusion.83
  632.0 25.2 %collective-permute-done.10 = bf16[1024,1024]{1,0:T(8,128)(2,1)} collective-permute-done((bf16[1024,1024]{1,0:T(8,128)(2,1)S(1)}, bf16[1024,1024]{1,0:T(8,128)(2,1)}, u32[]{:S(2)}, u32[]{:S(2)}) %collective-permute-start.10) | collective-permute-done | bytes 2097184 | tf_op jit(solution)/shard_map/ppermute | solution.py:38
  665.0 14.6 %reduce-scatter.15.cloned.1.call-done = bf16[128,256]{1,0:T(8,128)(2,1)} async-done(((bf16[1024,256]{1,0:T(8,128)(2,1)}), bf16[128,256]{1,0:T(8,128)(2,1)}) %reduce-scatter.15.cloned.1.call-update) | async-done | bytes 65552
  681.3 66.3 %reduce-scatter.13.cloned.1.call-done = bf16[128,768]{1,0:T(8,128)(2,1)} async-done(((bf16[1024,768]{1,0:T(8,128)(2,1)}), bf16[128,768]{1,0:T(8,128)(2,1)}) %reduce-scatter.13.cloned.1.call-update) | async-done | bytes 196624
  763.0 30.7 %all-gather.1 = f32[8,1,7680]{2,1,0:T(1,128)S(1)} all-gather(f32[1,1,7680]{2,1,0:T(1,128)S(1)} %reshape.251), channel_id=2, replica_groups=mesh['dp'=8,'mp'=4] {'dp'}, dimensions={0}, use_global_device_ids=true | all-gather | bytes 276480 | tf_op jit(solution)/shard_map/all_gather | solution.py:218
  794.6 12.3 %add_add_fusion.2 = f32[2048,1024]{1,0:T(8,128)} fusion(f32[2048,1024]{1,0:T(8,128)} %copy-done.9, bf16[2048,1024]{1,0:T(8,128)(2,1)} %param.19, f32[2048]{0:T(1024)S(1)} %negate_multiply_fusion.1, f32[2048]{0:T(1024)S(1)} %multiply_multiply_fusion.5, f32[1024]{0:T(1024)S(1)} %copy-done.45, f32[2048]{0:T(1024)S(1)} %copy-done.37, f32[2048]{0:T(1024)S(1)} %copy-done.35, ...), kind=kLoop, calls=%fused_computation.83 | loop fusion | flops 27262976 | bytes 25202688 | tf_op jit(solution)/shard_map/add | solution.py:195
  (322 shorter events, 362.7 us)
Async XLA Ops:
  7.2 177.0 %copy-start = (bf16[1024,1024]{1,0:T(8,128)(2,1)S(1)}, bf16[1024,1024]{1,0:T(8,128)(2,1)}, u32[]{:S(2)}) copy-start(bf16[1024,1024]{1,0:T(8,128)(2,1)} %param.28) | copy-start | bytes 6291460
  7.2 653.9 %reduce-scatter.17.cloned.1.call-start = ((), (), s32[]{:S(2)}) async-start(), calls=%async_computation.7 | async-start | bytes 2359296
  106.5 4.7 collective-permute-start
  114.4 58.2 %copy-start.38 = (f32[1024]{0:T(1024)S(1)}, f32[1024]{0:T(1024)}, u32[]{:S(2)}) copy-start(f32[1024]{0:T(1024)} %param.25) | copy-start | bytes 12292
  114.4 48.9 %collective-permute-start.1 = (bf16[1024,1024]{1,0:T(8,128)(2,1)S(1)}, bf16[1024,1024]{1,0:T(8,128)(2,1)S(1)}, u32[]{:S(2)}, u32[]{:S(2)}) collective-permute-start(bf16[1024,1024]{1,0:T(8,128)(2,1)S(1)} %add_convert_fusion.9), channel_id=1, source_target_pairs={{0,2},{1,3},{2,0},{3,1},{4,6},{5,7},{6,4},{7,5},{8,10},{9,11},{10,... | collective-permute-start | bytes 6291464 | tf_op jit(solution)/shard_map/ppermute | solution.py:38
  165.5 4.5 collective-permute-start.2
  184.3 25.6 %copy-start.21 = (f32[2048,1024]{1,0:T(8,128)}, f32[2048,1024]{1,0:T(8,128)S(1)}, u32[]{:S(2)}) copy-start(f32[2048,1024]{1,0:T(8,128)S(1)} %fusion.100) | copy-start | bytes 25165828
  230.6 18.3 %collective-permute-start.6 = (bf16[1024,1024]{1,0:T(8,128)(2,1)}, bf16[1024,1024]{1,0:T(8,128)(2,1)}, u32[]{:S(2)}, u32[]{:S(2)}) collective-permute-start(bf16[1024,1024]{1,0:T(8,128)(2,1)} %constant_dynamic-slice_fusion.3), channel_id=1, source_target_pairs={{0,1},{1,0},{2,3},{3,2},{4,5},{5,4},{6,7},{7,6},{8,9},{9,8},{10,11... | collective-permute-start | bytes 6291464 | tf_op jit(solution)/shard_map/ppermute | solution.py:36
  240.6 422.5 %reduce-scatter.11.cloned.1.call-start = ((), (), s32[]{:S(2)}) async-start(), calls=%async_computation.4 | async-start | bytes 2359296 | tf_op jit(solution)/shard_map/reduce_scatter | solution.py:198
  248.5 54.2 %copy-start.13 = (bf16[1024,1024]{1,0:T(8,128)(2,1)S(1)}, bf16[1024,1024]{1,0:T(8,128)(2,1)}, u32[]{:S(2)}) copy-start(bf16[1024,1024]{1,0:T(8,128)(2,1)} %copy-done.12) | copy-start | bytes 6291460
  248.5 5.2 collective-permute-start.3
  251.9 48.6 %collective-permute-start.7 = (bf16[1024,1024]{1,0:T(8,128)(2,1)S(1)}, bf16[1024,1024]{1,0:T(8,128)(2,1)S(1)}, u32[]{:S(2)}, u32[]{:S(2)}) collective-permute-start(bf16[1024,1024]{1,0:T(8,128)(2,1)S(1)} %add_convert_fusion.5), channel_id=1, source_target_pairs={{0,2},{1,3},{2,0},{3,1},{4,6},{5,7},{6,4},{7,5},{8,10},{9,11},{10,... | collective-permute-start | bytes 6291464 | tf_op jit(solution)/shard_map/ppermute | solution.py:38
  256.0 88.6 %collective-permute-start.4 = (bf16[1024,1024]{1,0:T(8,128)(2,1)}, bf16[1024,1024]{1,0:T(8,128)(2,1)}, u32[]{:S(2)}, u32[]{:S(2)}) collective-permute-start(bf16[1024,1024]{1,0:T(8,128)(2,1)} %add_convert_fusion.7), channel_id=1, source_target_pairs={{0,2},{1,3},{2,0},{3,1},{4,6},{5,7},{6,4},{7,5},{8,10},{9,11},{10,... | collective-permute-start | bytes 6291464 | tf_op jit(solution)/shard_map/ppermute | solution.py:38
  302.7 45.2 %collective-permute-start.8 = (bf16[1024,1024]{1,0:T(8,128)(2,1)}, bf16[1024,1024]{1,0:T(8,128)(2,1)}, u32[]{:S(2)}, u32[]{:S(2)}) collective-permute-start(bf16[1024,1024]{1,0:T(8,128)(2,1)} %add_convert_fusion.4), channel_id=1, source_target_pairs={{0,1},{1,0},{2,3},{3,2},{4,5},{5,4},{6,7},{7,6},{8,9},{9,8},{10,11... | collective-permute-start | bytes 6291464 | tf_op jit(solution)/shard_map/ppermute | solution.py:40
  313.8 365.8 %reduce-scatter.15.cloned.1.call-start = ((), (), s32[]{:S(2)}) async-start(), calls=%async_computation.6 | async-start | bytes 589824
  314.0 36.5 %copy-start.4 = (bf16[2048,1024]{1,0:T(8,128)(2,1)S(1)}, bf16[2048,1024]{1,0:T(8,128)(2,1)}, u32[]{:S(2)}) copy-start(bf16[2048,1024]{1,0:T(8,128)(2,1)} %param.19) | copy-start | bytes 12582916
  314.0 36.5 %copy-start.15 = (bf16[1024,1024]{1,0:T(8,128)(2,1)S(1)}, bf16[1024,1024]{1,0:T(8,128)(2,1)}, u32[]{:S(2)}) copy-start(bf16[1024,1024]{1,0:T(8,128)(2,1)} %copy-done.14) | copy-start | bytes 6291460
  347.8 18.7 %collective-permute-start.5 = (bf16[1024,1024]{1,0:T(8,128)(2,1)S(1)}, bf16[1024,1024]{1,0:T(8,128)(2,1)S(1)}, u32[]{:S(2)}, u32[]{:S(2)}) collective-permute-start(bf16[1024,1024]{1,0:T(8,128)(2,1)S(1)} %add_convert_fusion.6), channel_id=1, source_target_pairs={{0,1},{1,0},{2,3},{3,2},{4,5},{5,4},{6,7},{7,6},{8,9},{9,8},{10,11... | collective-permute-start | bytes 6291464 | tf_op jit(solution)/shard_map/ppermute | solution.py:40
  603.8 4.3 collective-permute-start.9
  609.1 48.1 %collective-permute-start.10 = (bf16[1024,1024]{1,0:T(8,128)(2,1)S(1)}, bf16[1024,1024]{1,0:T(8,128)(2,1)}, u32[]{:S(2)}, u32[]{:S(2)}) collective-permute-start(bf16[1024,1024]{1,0:T(8,128)(2,1)S(1)} %add_convert_fusion.3), channel_id=1, source_target_pairs={{0,2},{1,3},{2,0},{3,1},{4,6},{5,7},{6,4},{7,5},{8,10},{9,11},{10,... | collective-permute-start | bytes 6291464 | tf_op jit(solution)/shard_map/ppermute | solution.py:38
  616.6 131.0 %reduce-scatter.13.cloned.1.call-start = ((), (), s32[]{:S(2)}) async-start(), calls=%async_computation.5 | async-start | bytes 1769472
  632.0 119.7 %copy-start.35 = (f32[2048]{0:T(1024)S(1)}, f32[2048]{0:T(1024)}, u32[]{:S(2)}) copy-start(f32[2048]{0:T(1024)} %copy-done.34) | copy-start | bytes 24580
  632.0 119.7 %copy-start.45 = (f32[1024]{0:T(1024)S(1)}, f32[1024]{0:T(1024)}, u32[]{:S(2)}) copy-start(f32[1024]{0:T(1024)} %param.30) | copy-start | bytes 12292
  661.1 88.6 %collective-permute-start.11 = (bf16[1024,1024]{1,0:T(8,128)(2,1)}, bf16[1024,1024]{1,0:T(8,128)(2,1)S(1)}, u32[]{:S(2)}, u32[]{:S(2)}) collective-permute-start(bf16[1024,1024]{1,0:T(8,128)(2,1)} %add_convert_fusion.2), channel_id=1, source_target_pairs={{0,1},{1,0},{2,3},{3,2},{4,5},{5,4},{6,7},{7,6},{8,9},{9,8},{10,11... | collective-permute-start | bytes 6291464 | tf_op jit(solution)/shard_map/ppermute | solution.py:40
  (65 other events, 488.7 us)
Sparse Core Ops, SparseCore 0:
  240.7 69.8 reduce-scatter.16
  314.1 69.8 reduce-scatter.10
  616.7 62.8 reduce-scatter.14
  682.9 64.5 reduce-scatter.12
